TPU v7x, 128 devices: a whole 4x4x4 slice. The times are simulated.
128 devices in a mesh: dp: 32 (over x, z, core), tensor: 4 (over y).
Axes of the slice: x: 4, y: 4, z: 4, core: 2. Of those that a mesh axis runs over, the one named last changes fastest.
Arguments:
- tokens: bfloat16 [2, 2048, 4096], P(None, 'dp', 'tensor'), may hold values from -6 to 6
- routes: int32 [2, 2048, 2], P(None, 'dp'), may hold values from 0 to 7, all different within a row; in each aligned block of 64 rows (0 to 63, 64 to 127, ..., all dimensions but the last counted through in order) at most 20 rows name the same one
- probs: float32 [2, 2048, 8], P(None, 'dp'), may hold values from 0 to 1, as said below
- w_gate: bfloat16 [32, 4096, 3584], P('dp', None, 'tensor'), may hold values from -0.09375 to 0.09375
- w_up: bfloat16 [32, 4096, 3584], P('dp', None, 'tensor'), may hold values from -0.09375 to 0.09375
- w_down: bfloat16 [32, 3584, 4096], P('dp', 'tensor'), may hold values from -0.046875 to 0.046875
Outputs:
- mixed: bfloat16 [2, 2048, 4096], P(None, 'dp', 'tensor')
- aux_loss: float32 [2, 8], replicated
Inputs may be any that keep to these rules, and one draw needn't show every extreme that they name: `routes`: in each aligned block of 64 rows (the rows of one index of dp in one micro-batch) no expert is named in more than 20 entries; the 2 experts of a row differ. `probs`: each row is positive and sums to one.
All inputs are finite; a program needn't handle non-finite values.
Results may differ from a plain program's by a relative error of at most 0.012.
Values may be sent and summed in bfloat16 or wider, within the bound.
A program may use at most 128 MiB of HBM per device.

v0:
```python
import jax
import jax.numpy as jnp
from jax import lax
from jax.sharding import PartitionSpec as P

MICRO = 2
CAP = 20


def together(arrays, axis):
    ravelled, at, gathered = (jnp.concatenate([a.reshape(-1) for a in arrays]), 0, [])
    subtotal = lax.psum(ravelled, axis)
    for a in arrays:
        gathered.append(subtotal[at : at + a.size].reshape(a.shape))
        at += a.size
    return tuple(gathered)


def slot_tables(route, prob):
    rows_count = route.shape[0]
    experts = prob.shape[-1]
    capacity = CAP
    flat = route.reshape(-1)
    onehot = (flat[:, None] == jnp.arange(experts, dtype=jnp.int32)[None, :]).astype(jnp.int32)
    before = jnp.cumsum(onehot, axis=0) - onehot
    place = jnp.sum(before * onehot, axis=1)
    slot = flat * capacity + place
    picked = jnp.take_along_axis(prob, route, axis=1)
    weights = picked / jnp.sum(picked, axis=1, keepdims=True)
    grid = (slot[:, None] == jnp.arange(experts * capacity, dtype=jnp.int32)[None, :]).astype(
        jnp.float32
    )
    grid = grid.reshape(rows_count, route.shape[1], experts * capacity)
    dispatch = jnp.sum(grid, axis=1).T.astype(jnp.bfloat16)
    combine = jnp.sum(grid * weights[:, :, None], axis=1)
    counts = jnp.sum(onehot, axis=0).astype(jnp.float32)
    return (dispatch, combine, counts)


def spread_slots(slots, experts, copies_per, capacity):
    width = slots.shape[-1]
    wide = jnp.broadcast_to(
        slots.reshape(experts, 1, capacity, width), (experts, copies_per, capacity, width)
    )
    return wide.reshape(experts * copies_per, capacity, width)


def local(tokens, routes, probs, w_gate, w_up, w_down):
    groups = lax.axis_size("dp")
    experts = probs.shape[-1]
    copies_per = groups // experts
    capacity = CAP
    gate_local = w_gate[0]
    up_local = w_up[0]
    down_local = w_down[0]
    rows_local = tokens.shape[1]
    total_rows = rows_local * groups
    top_count = routes.shape[-1]
    tables = [slot_tables(routes[index], probs[index]) for index in range(MICRO)]
    prob_local = [jnp.sum(probs[index], axis=0) for index in range(MICRO)]
    count_table, prob_table = together(
        (jnp.stack([tables[index][2] for index in range(MICRO)]), jnp.stack(prob_local)), "dp"
    )
    outputs = []
    loss_terms = []
    for micro_index in range(MICRO):
        dispatch, combine, counts = tables[micro_index]
        count_all = count_table[micro_index]
        prob_all = prob_table[micro_index]
        width_local = tokens.shape[2]
        slots = jnp.dot(dispatch, tokens[micro_index], preferred_element_type=jnp.float32).astype(
            jnp.bfloat16
        )
        arrived = lax.all_to_all(
            spread_slots(slots, experts, copies_per, capacity),
            "dp",
            split_axis=0,
            concat_axis=0,
            tiled=True,
        )
        piece = lax.all_gather(arrived, "tensor", axis=2, tiled=True)
        piece_rows = piece.reshape(-1, piece.shape[2])
        gate = jnp.dot(piece_rows, gate_local, preferred_element_type=jnp.float32)
        up = jnp.dot(piece_rows, up_local, preferred_element_type=jnp.float32)
        hidden = (jax.nn.silu(gate) * up).astype(jnp.bfloat16)
        part = jnp.dot(hidden, down_local, preferred_element_type=jnp.float32).astype(jnp.bfloat16)
        reduced = lax.psum_scatter(part, "tensor", scatter_dimension=1, tiled=True).astype(
            jnp.float32
        )
        returned = lax.all_to_all(
            reduced.reshape(groups, capacity, width_local).astype(jnp.bfloat16),
            "dp",
            split_axis=0,
            concat_axis=0,
            tiled=True,
        ).astype(jnp.float32)
        summed = jnp.sum(returned.reshape(experts, copies_per, capacity, width_local), axis=1)
        mixed = jnp.dot(
            combine,
            summed.reshape(experts * capacity, width_local),
            precision=lax.Precision.HIGHEST,
            preferred_element_type=jnp.float32,
        )
        outputs.append(mixed.astype(jnp.bfloat16))
        loss_terms.append(
            experts * (count_all / (total_rows * top_count)) * (prob_all / total_rows)
        )
    return (jnp.stack(outputs), jnp.stack(loss_terms))


def solution(mesh):
    in_specs = (
        P(None, "dp", "tensor"),
        P(None, "dp", None),
        P(None, "dp", None),
        P("dp", None, "tensor"),
        P("dp", None, "tensor"),
        P("dp", "tensor", None),
    )
    out_specs = (P(None, "dp", "tensor"), P())
    return jax.shard_map(local, mesh=mesh, in_specs=in_specs, out_specs=out_specs, check_vma=False)
```

profile of v0, /device:TPU:1, one launch (start us, length us, event | category | flops | bytes accessed | tf_op | source)
XLA Modules:
  0.0 393.9 jit_solution(13326397115779215763)
XLA Ops:
  7.9 0.7 bitcast_or_fusion.1
  10.4 0.9 slice_reduce_fusion.1
  11.5 1.0 gather_fusion
  13.0 1.0 gather_fusion.1
  15.0 32.2 %all_to_all.20 = bf16[32,20,1024]{2,1,0:T(8,128)(2,1)} all-to-all(bf16[32,20,1024]{2,1,0:T(8,128)(2,1)S(1)} %bitcast.97), channel_id=1, replica_groups=mesh['dp'=32,'tensor'=4] {'dp'}, dimensions={0} | all-to-all | bytes 2621440 | tf_op jit(solution)/shard_map/all_to_all | solution.py:74
  47.8 26.4 %all_to_all.21 = bf16[32,20,1024]{2,1,0:T(8,128)(2,1)} all-to-all(bf16[32,20,1024]{2,1,0:T(8,128)(2,1)S(1)} %bitcast.98), channel_id=1, replica_groups=mesh['dp'=32,'tensor'=4] {'dp'}, dimensions={0} | all-to-all | bytes 2621440 | tf_op jit(solution)/shard_map/all_to_all | solution.py:74
  74.2 36.0 %all-gather.5.cloned.1.call-done = bf16[32,20,4096]{2,1,0:T(8,128)(2,1)} async-done(((bf16[32,20,1024]{2,1,0:T(8,128)(2,1)}), bf16[32,20,4096]{2,1,0:T(8,128)(2,1)}) %all-gather.5.cloned.1.call-update) | async-done | bytes 5242896 | tf_op jit(solution)/shard_map/all_gather | solution.py:81
  110.3 7.8 %reshape.140 = bf16[640,4096]{1,0:T(8,128)(2,1)} reshape(bf16[32,20,4096]{2,1,0:T(8,128)(2,1)} %all-gather.5.cloned.1.call-done) | data formatting | bytes 10485760 | tf_op jit(solution)/shard_map/reshape | solution.py:82
  118.0 11.7 %fusion.8 = f32[640,896]{1,0:T(8,128)S(1)} fusion(bf16[640,4096]{1,0:T(8,128)(2,1)} %reshape.140, bf16[1,4096,896]{2,1,0:T(8,128)(2,1)} %param.11), kind=kOutput, calls=%fused_computation.10 | convolution fusion | flops 4697620480 | bytes 14876672 | tf_op jit(solution)/shard_map/dot_general | solution.py:83
  129.7 18.9 %fusion.15 = bf16[640,4096]{1,0:T(8,128)(2,1)} fusion(bf16[1,896,4096]{2,1,0:T(8,128)(2,1)} %param.13, f32[640,896]{1,0:T(8,128)S(1)} %fusion.8, bf16[640,4096]{1,0:T(8,128)(2,1)} %reshape.140, bf16[1,4096,896]{2,1,0:T(8,128)(2,1)} %param.12), kind=kOutput, calls=%fused_computation.15 | convolution fusion | flops 9401303040 | bytes 27459584 | tf_op jit(solution)/shard_map/dot_general | solution.py:86
  148.8 29.4 %all-gather.3.cloned.1.call-done = bf16[32,20,4096]{2,1,0:T(8,128)(2,1)} async-done(((bf16[32,20,1024]{2,1,0:T(8,128)(2,1)}), bf16[32,20,4096]{2,1,0:T(8,128)(2,1)}) %all-gather.3.cloned.1.call-update) | async-done | bytes 5242896 | tf_op jit(solution)/shard_map/all_gather | solution.py:81
  178.2 7.7 %reshape.135 = bf16[640,4096]{1,0:T(8,128)(2,1)} reshape(bf16[32,20,4096]{2,1,0:T(8,128)(2,1)} %all-gather.3.cloned.1.call-done) | data formatting | bytes 10485760 | tf_op jit(solution)/shard_map/reshape | solution.py:82
  185.9 11.6 %fusion.10 = f32[640,896]{1,0:T(8,128)S(1)} fusion(bf16[640,4096]{1,0:T(8,128)(2,1)} %reshape.135, bf16[1,4096,896]{2,1,0:T(8,128)(2,1)} %param.11), kind=kOutput, calls=%fused_computation.12 | convolution fusion | flops 4697620480 | bytes 14876672 | tf_op jit(solution)/shard_map/dot_general | solution.py:83
  197.5 18.9 %fusion.12 = bf16[640,4096]{1,0:T(8,128)(2,1)} fusion(bf16[1,896,4096]{2,1,0:T(8,128)(2,1)} %param.13, f32[640,896]{1,0:T(8,128)S(1)} %fusion.10, bf16[640,4096]{1,0:T(8,128)(2,1)} %reshape.135, bf16[1,4096,896]{2,1,0:T(8,128)(2,1)} %param.12), kind=kOutput, calls=%fused_computation.14 | convolution fusion | flops 9401303040 | bytes 27459584 | tf_op jit(solution)/shard_map/dot_general | solution.py:86
  216.4 20.4 %reduce-scatter.5.cloned.1.call-done = bf16[640,1024]{1,0:T(8,128)(2,1)} async-done(((bf16[640,4096]{1,0:T(8,128)(2,1)}), bf16[640,1024]{1,0:T(8,128)(2,1)}) %reduce-scatter.5.cloned.1.call-update) | async-done | bytes 1310736 | tf_op jit(solution)/shard_map/reduce_scatter | solution.py:87
  236.8 3.2 convert_element_type.98
  240.0 7.7 %all-to-all-start.3 = ((bf16[32,20,1024]{2,1,0:T(8,128)(2,1)}), bf16[32,20,1024]{2,1,0:T(8,128)(2,1)S(1)}, u32[]{:S(2)}, u32[]{:S(2)}) async-start(bf16[32,20,1024]{2,1,0:T(8,128)(2,1)} %convert_element_type.98), calls=%async_computation.5 | async-start | bytes 3145728 | tf_op jit(solution)/shard_map/all_to_all | solution.py:90
  247.7 46.5 %reduce-scatter.3.cloned.1.call-done = bf16[640,1024]{1,0:T(8,128)(2,1)} async-done(((bf16[640,4096]{1,0:T(8,128)(2,1)}), bf16[640,1024]{1,0:T(8,128)(2,1)}) %reduce-scatter.3.cloned.1.call-update) | async-done | bytes 1310736 | tf_op jit(solution)/shard_map/reduce_scatter | solution.py:87
  294.3 3.2 convert_element_type.90
  297.5 7.7 %all-to-all-start.1 = ((bf16[32,20,1024]{2,1,0:T(8,128)(2,1)}), bf16[32,20,1024]{2,1,0:T(8,128)(2,1)S(1)}, u32[]{:S(2)}, u32[]{:S(2)}) async-start(bf16[32,20,1024]{2,1,0:T(8,128)(2,1)} %convert_element_type.90), calls=%async_computation.2 | async-start | bytes 3145728 | tf_op jit(solution)/shard_map/all_to_all | solution.py:90
  305.5 76.7 %psum.7 = f32[32]{0:T(128)S(1)} all-reduce(f32[32]{0:T(128)S(1)} %pad_maximum_fusion.4), channel_id=1, replica_groups=mesh['dp'=32,'tensor'=4] {'dp'}, use_global_device_ids=true, to_apply=%region_18.20 | all-reduce | flops 32 | bytes 256 | tf_op jit(solution)/shard_map/psum | solution.py:12
  382.9 1.2 convert_reduce_fusion
  384.0 1.2 reshape.143
  386.6 0.7 pad_maximum_fusion
  (60 shorter events, 7.3 us)
Async XLA Ops:
  7.2 103.1 %all-gather.5.cloned.1.call-start = ((), (), s32[]{:S(2)}) async-start(), calls=%async_computation.8 | async-start | bytes 7864320 | tf_op jit(solution)/shard_map/all_gather | solution.py:81
  13.0 1.3 copy-start.1
  13.0 1.5 copy-start
  47.2 131.0 %all-gather.3.cloned.1.call-start = ((), (), s32[]{:S(2)}) async-start(), calls=%async_computation.6 | async-start | bytes 7864320 | tf_op jit(solution)/shard_map/all_gather | solution.py:81
  74.2 162.6 %reduce-scatter.5.cloned.1.call-start = ((), (), s32[]{:S(2)}) async-start(), calls=%async_computation.9 | async-start | bytes 6553600 | tf_op jit(solution)/shard_map/reduce_scatter | solution.py:87
  148.6 145.7 %reduce-scatter.3.cloned.1.call-start = ((), (), s32[]{:S(2)}) async-start(), calls=%async_computation.7 | async-start | bytes 6553600 | tf_op jit(solution)/shard_map/reduce_scatter | solution.py:87
  240.0 57.5 %all-to-all-start.3 = ((bf16[32,20,1024]{2,1,0:T(8,128)(2,1)}), bf16[32,20,1024]{2,1,0:T(8,128)(2,1)S(1)}, u32[]{:S(2)}, u32[]{:S(2)}) async-start(bf16[32,20,1024]{2,1,0:T(8,128)(2,1)} %convert_element_type.98), calls=%async_computation.5 | async-start | bytes 3145728 | tf_op jit(solution)/shard_map/all_to_all | solution.py:90
  297.5 87.7 %all-to-all-start.1 = ((bf16[32,20,1024]{2,1,0:T(8,128)(2,1)}), bf16[32,20,1024]{2,1,0:T(8,128)(2,1)S(1)}, u32[]{:S(2)}, u32[]{:S(2)}) async-start(bf16[32,20,1024]{2,1,0:T(8,128)(2,1)} %convert_element_type.90), calls=%async_computation.2 | async-start | bytes 3145728 | tf_op jit(solution)/shard_map/all_to_all | solution.py:90
Sparse Core Ops, SparseCore 0:
  47.3 62.8 all-gather.4
  111.9 66.2 all-gather.2
  180.6 56.1 reduce-scatter.4
  239.1 55.1 reduce-scatter.2
where the time goes:
time: 395 us; the launch traced here: 394 us
  blocking collectives  135 us (34%)
  waiting for transfers between devices  132 us (33%)
  matrix products  62.5 us (16%)
  local copies, waits for them, and re-layouts  28.3 us (7%)
  starting transfers between devices  15.8 us (4%)
  between operations  14 us (4%)
  other arithmetic  5.56 us (1%)
    psum x1, blocking collectives, together(): subtotal = lax.psum(ravelled, axis)  76.7 us
    reduce_scatter x2, waiting for transfers between devices, local(): lax.psum_scatter(part, 'tensor', scatter_dimension=1, tiled=True)  67 us
    all_gather x2, waiting for transfers between devices, local(): piece = lax.all_gather(arrived, 'tensor', axis=2, tiled=True)  65.4 us
    all_to_all x2, blocking collectives, local(): lax.all_to_all(spread_slots(slots, experts, copies_per, capacity), 'dp',...  58.5 us
    dot_general x2, matrix products, local(): jnp.dot(hidden, down_local, preferred_element_type=jnp.float32)  37.8 us
    dot_general x2, matrix products, local(): gate = jnp.dot(piece_rows, gate_local, preferred_element_type=jnp.float32)  23.2 us
    all_to_all x2, starting transfers between devices, local(): lax.all_to_all(reduced.reshape(groups, capacity, width_local).astype(jnp....  15.4 us
    reshape x2, local copies, waits for them, and re-layouts, local(): piece_rows = piece.reshape(-1, piece.shape[2])  15.4 us
  transfers between devices with their start and end apart: 6, of which 4 were waited for; matrix products, arithmetic and copies ran while one was open for 22% of the time, Pallas kernels for 0%

commit v1 on v0

--- a/solution.py
+++ b/solution.py
@@ -78,7 +78,15 @@
             concat_axis=0,
             tiled=True,
         )
-        piece = lax.all_gather(arrived, "tensor", axis=2, tiled=True)
+        world_n = lax.axis_size("tensor")
+        steps_seen = tuple(((no, (no + 1) % world_n) for no in range(world_n)))
+        state_next = [None] * world_n
+        state_next[world_n - 1] = arrived
+        for j0 in range(world_n - 2, -1, -1):
+            state_next[j0] = lax.ppermute(state_next[j0 + 1], axis_name="tensor", perm=steps_seen)
+        carry = jnp.concatenate(state_next, axis=2)
+        wide_out = (lax.axis_index("tensor") + 1) * arrived.shape[2]
+        piece = jnp.roll(carry, wide_out, axis=2)
         piece_rows = piece.reshape(-1, piece.shape[2])
         gate = jnp.dot(piece_rows, gate_local, preferred_element_type=jnp.float32)
         up = jnp.dot(piece_rows, up_local, preferred_element_type=jnp.float32)

time: 395 us -> 478 us (1.21)
  waiting for transfers between devices: 132 us -> 175 us
  other arithmetic: 5.56 us -> 29.6 us
  local copies, waits for them, and re-layouts: 28.3 us -> 42 us
    ppermute x0 -> x6, waiting for transfers between devices: none -> 134 us  [local(): lax.ppermute(state_next[j0 + 1], axis_name='tensor', perm=steps_seen)]
    all_gather x2 -> x0, waiting for transfers between devices: 65.4 us -> none  [local(): piece = lax.all_gather(arrived, 'tensor', axis=2, tiled=True)]
    reduce_scatter x2, waiting for transfers between devices: 67 us -> 41.4 us  [local(): lax.psum_scatter(part, 'tensor', scatter_dimension=1, tiled=True)]
    concatenate x0 -> x2, other arithmetic: none -> 24 us  [local(): piece = jnp.roll(carry, wide_out, axis=2)]
    ppermute x0 -> x6, local copies, waits for them, and re-layouts: none -> 11 us  [local(): lax.ppermute(state_next[j0 + 1], axis_name='tensor', perm=steps_seen)]
  transfers between devices with their start and end apart: 6 -> 10, of which waited for: 4 -> 6; matrix products, arithmetic and copies ran while one was open for 22% -> 26% of each run, Pallas kernels for 0% -> 0%
where the time goes in v1:
time: 478 us; the launch traced here: 477 us
  waiting for transfers between devices  175 us (37%)
  blocking collectives  136 us (28%)
  matrix products  61.7 us (13%)
  local copies, waits for them, and re-layouts  42 us (9%)
  other arithmetic  29.6 us (6%)
  starting transfers between devices  18.6 us (4%)
  between operations  14.4 us (3%)
    ppermute x6, waiting for transfers between devices, local(): lax.ppermute(state_next[j0 + 1], axis_name='tensor', perm=steps_seen)  134 us
    psum x1, blocking collectives, together(): subtotal = lax.psum(ravelled, axis)  76.7 us
    all_to_all x2, blocking collectives, local(): lax.all_to_all(spread_slots(slots, experts, copies_per, capacity), 'dp',...  58.9 us
    reduce_scatter x2, waiting for transfers between devices, local(): lax.psum_scatter(part, 'tensor', scatter_dimension=1, tiled=True)  41.4 us
    dot_general x2, matrix products, local(): jnp.dot(hidden, down_local, preferred_element_type=jnp.float32)  37.8 us
    concatenate x2, other arithmetic, local(): piece = jnp.roll(carry, wide_out, axis=2)  24 us
    dot_general x2, matrix products, local(): gate = jnp.dot(piece_rows, gate_local, preferred_element_type=jnp.float32)  22.4 us
    reshape x2, local copies, waits for them, and re-layouts, local(): piece_rows = piece.reshape(-1, piece.shape[2])  15.6 us
  transfers between devices with their start and end apart: 10, of which 6 were waited for; matrix products, arithmetic and copies ran while one was open for 26% of the time, Pallas kernels for 0%

profile of v1, /device:TPU:1, one launch (start us, length us, event | category | flops | bytes accessed | tf_op | source)
XLA Modules:
  0.0 477.3 jit_solution(12313451920789929633)
XLA Ops:
  15.0 32.0 %all_to_all.20 = bf16[32,20,1024]{2,1,0:T(8,128)(2,1)S(1)} all-to-all(bf16[32,20,1024]{2,1,0:T(8,128)(2,1)S(1)} %bitcast.97), channel_id=1, replica_groups=mesh['dp'=32,'tensor'=4] {'dp'}, dimensions={0} | all-to-all | bytes 2621440 | tf_op jit(solution)/shard_map/all_to_all | solution.py:74
  49.2 30.7 %collective-permute-done.3 = bf16[32,20,1024]{2,0,1:T(8,128)(2,1)} collective-permute-done((bf16[32,20,1024]{2,0,1:T(8,128)(2,1)S(1)}, bf16[32,20,1024]{2,0,1:T(8,128)(2,1)}, u32[]{:S(2)}, u32[]{:S(2)}) %collective-permute-start.3) | collective-permute-done | bytes 1310752 | tf_op jit(solution)/shard_map/ppermute | solution.py:86
  80.4 26.8 %all_to_all.21 = bf16[32,20,1024]{2,1,0:T(8,128)(2,1)S(1)} all-to-all(bf16[32,20,1024]{2,1,0:T(8,128)(2,1)S(1)} %bitcast.98), channel_id=1, replica_groups=mesh['dp'=32,'tensor'=4] {'dp'}, dimensions={0} | all-to-all | bytes 2621440 | tf_op jit(solution)/shard_map/all_to_all | solution.py:74
  111.4 2.0 copy.83
  113.5 27.7 %collective-permute-done = bf16[32,20,1024]{2,0,1:T(8,128)(2,1)} collective-permute-done((bf16[32,20,1024]{2,0,1:T(8,128)(2,1)}, bf16[32,20,1024]{2,0,1:T(8,128)(2,1)}, u32[]{:S(2)}, u32[]{:S(2)}) %collective-permute-start) | collective-permute-done | bytes 1310752 | tf_op jit(solution)/shard_map/ppermute | solution.py:86
  141.3 2.0 copy.82
  143.3 25.9 %collective-permute-done.5 = bf16[32,20,1024]{2,0,1:T(8,128)(2,1)} collective-permute-done((bf16[32,20,1024]{2,0,1:T(8,128)(2,1)}, bf16[32,20,1024]{2,0,1:T(8,128)(2,1)}, u32[]{:S(2)}, u32[]{:S(2)}) %collective-permute-start.5) | collective-permute-done | bytes 1310752 | tf_op jit(solution)/shard_map/ppermute | solution.py:86
  169.3 2.1 copy.81
  171.3 11.9 %fusion.21 = bf16[32,20,4096]{2,1,0:T(8,128)(2,1)} fusion(s32[]{:T(128)S(6)} %select_n.23, bf16[32,20,1024]{2,1,0:T(8,128)(2,1)S(1)} %copy.81, bf16[32,20,1024]{2,1,0:T(8,128)(2,1)S(1)} %copy.82, bf16[32,20,1024]{2,1,0:T(8,128)(2,1)S(1)} %copy.83, bf16[32,20,1024]{2,1,0:T(8,128)(2,1)S(1)} %all_to_all.20), kind=kLoop, calls=%fused_computation.35 | loop fusion | flops 41943040 | bytes 10485764 | tf_op jit(solution)/shard_map/jit(_roll_dynamic)/concatenate | solution.py:89
  183.2 7.8 %reshape.140 = bf16[640,4096]{1,0:T(8,128)(2,1)} reshape(bf16[32,20,4096]{2,1,0:T(8,128)(2,1)} %fusion.21) | data formatting | bytes 10485760 | tf_op jit(solution)/shard_map/reshape | solution.py:90
  191.1 10.7 %fusion.8 = f32[640,896]{1,0:T(8,128)} fusion(bf16[640,4096]{1,0:T(8,128)(2,1)} %reshape.140, bf16[1,4096,896]{2,1,0:T(8,128)(2,1)} %param.13), kind=kOutput, calls=%fused_computation.26 | convolution fusion | flops 4697620480 | bytes 14876672 | tf_op jit(solution)/shard_map/dot_general | solution.py:91
  201.7 19.1 %fusion.15 = bf16[640,4096]{1,0:T(8,128)(2,1)} fusion(bf16[1,896,4096]{2,1,0:T(8,128)(2,1)} %param.15, f32[640,896]{1,0:T(8,128)} %fusion.8, bf16[640,4096]{1,0:T(8,128)(2,1)} %reshape.140, bf16[1,4096,896]{2,1,0:T(8,128)(2,1)} %param.14), kind=kOutput, calls=%fused_computation.31 | convolution fusion | flops 9401303040 | bytes 27459584 | tf_op jit(solution)/shard_map/dot_general | solution.py:94
  223.1 2.1 copy.74
  225.2 48.7 %collective-permute-done.2 = bf16[32,20,1024]{2,0,1:T(8,128)(2,1)S(1)} collective-permute-done((bf16[32,20,1024]{2,0,1:T(8,128)(2,1)}, bf16[32,20,1024]{2,0,1:T(8,128)(2,1)S(1)}, u32[]{:S(2)}, u32[]{:S(2)}) %collective-permute-start.2) | collective-permute-done | bytes 1310752 | tf_op jit(solution)/shard_map/ppermute | solution.py:86
  274.6 12.1 %fusion.28 = bf16[32,20,4096]{2,1,0:T(8,128)(2,1)} fusion(s32[]{:T(128)S(6)} %select_n.23, bf16[32,20,1024]{2,1,0:T(8,128)(2,1)S(1)} %copy.73, bf16[32,20,1024]{2,1,0:T(8,128)(2,1)S(1)} %copy.74, bf16[32,20,1024]{2,1,0:T(8,128)(2,1)S(1)} %copy.75, bf16[32,20,1024]{2,1,0:T(8,128)(2,1)S(1)} %all_to_all.21), kind=kLoop, calls=%fused_computation.42 | loop fusion | flops 41943040 | bytes 10485764 | tf_op jit(solution)/shard_map/jit(_roll_dynamic)/concatenate | solution.py:89
  286.8 7.8 %reshape.135 = bf16[640,4096]{1,0:T(8,128)(2,1)} reshape(bf16[32,20,4096]{2,1,0:T(8,128)(2,1)} %fusion.28) | data formatting | bytes 10485760 | tf_op jit(solution)/shard_map/reshape | solution.py:90
  294.5 11.7 %fusion.10 = f32[640,896]{1,0:T(8,128)S(1)} fusion(bf16[640,4096]{1,0:T(8,128)(2,1)} %reshape.135, bf16[1,4096,896]{2,1,0:T(8,128)(2,1)} %param.13), kind=kOutput, calls=%fused_computation.28 | convolution fusion | flops 4697620480 | bytes 14876672 | tf_op jit(solution)/shard_map/dot_general | solution.py:91
  306.2 18.7 %fusion.12 = bf16[640,4096]{1,0:T(8,128)(2,1)} fusion(bf16[1,896,4096]{2,1,0:T(8,128)(2,1)} %param.15, f32[640,896]{1,0:T(8,128)S(1)} %fusion.10, bf16[640,4096]{1,0:T(8,128)(2,1)} %reshape.135, bf16[1,4096,896]{2,1,0:T(8,128)(2,1)} %param.14), kind=kOutput, calls=%fused_computation.30 | convolution fusion | flops 9401303040 | bytes 27459584 | tf_op jit(solution)/shard_map/dot_general | solution.py:94
  325.0 3.2 convert_element_type.98
  328.2 7.7 %all-to-all-start.3 = ((bf16[32,20,1024]{2,1,0:T(8,128)(2,1)}), bf16[32,20,1024]{2,1,0:T(8,128)(2,1)S(1)}, u32[]{:S(2)}, u32[]{:S(2)}) async-start(bf16[32,20,1024]{2,1,0:T(8,128)(2,1)} %convert_element_type.98), calls=%async_computation.5 | async-start | bytes 3145728 | tf_op jit(solution)/shard_map/all_to_all | solution.py:98
  336.0 41.4 %reduce-scatter.3.cloned.1.call-done = bf16[640,1024]{1,0:T(8,128)(2,1)} async-done(((bf16[640,4096]{1,0:T(8,128)(2,1)}), bf16[640,1024]{1,0:T(8,128)(2,1)}) %reduce-scatter.3.cloned.1.call-update) | async-done | bytes 1310736 | tf_op jit(solution)/shard_map/reduce_scatter | solution.py:95
  377.4 3.2 convert_element_type.90
  380.6 7.7 %all-to-all-start.1 = ((bf16[32,20,1024]{2,1,0:T(8,128)(2,1)}), bf16[32,20,1024]{2,1,0:T(8,128)(2,1)S(1)}, u32[]{:S(2)}, u32[]{:S(2)}) async-start(bf16[32,20,1024]{2,1,0:T(8,128)(2,1)} %convert_element_type.90), calls=%async_computation.2 | async-start | bytes 3145728 | tf_op jit(solution)/shard_map/all_to_all | solution.py:98
  388.6 76.7 %psum.7 = f32[32]{0:T(128)S(1)} all-reduce(f32[32]{0:T(128)S(1)} %pad_maximum_fusion.4), channel_id=1, replica_groups=mesh['dp'=32,'tensor'=4] {'dp'}, use_global_device_ids=true, to_apply=%region_18.21 | all-reduce | flops 32 | bytes 256 | tf_op jit(solution)/shard_map/psum | solution.py:12
  (76 shorter events, 22.9 us)
Async XLA Ops:
  7.2 317.8 %reduce-scatter.5.cloned.1.call-start = ((), (), s32[]{:S(2)}) async-start(), calls=%async_computation.7 | async-start | bytes 6553600 | tf_op jit(solution)/shard_map/reduce_scatter | solution.py:95
  13.0 1.3 copy-start.1
  13.0 1.5 copy-start
  47.8 32.1 %collective-permute-start.3 = (bf16[32,20,1024]{2,0,1:T(8,128)(2,1)S(1)}, bf16[32,20,1024]{2,0,1:T(8,128)(2,1)}, u32[]{:S(2)}, u32[]{:S(2)}) collective-permute-start(bf16[32,20,1024]{2,0,1:T(8,128)(2,1)S(1)} %copy.80), channel_id=1, source_target_pairs={{0,1},{1,2},{2,3},{3,0},{4,5},{5,6},{6,7},{7,4},{8,9},{9,10},{10,1... | collective-permute-start | bytes 3932168 | tf_op jit(solution)/shard_map/ppermute | solution.py:86
  79.9 31.3 %collective-permute-start.4 = (bf16[32,20,1024]{2,0,1:T(8,128)(2,1)}, bf16[32,20,1024]{2,0,1:T(8,128)(2,1)}, u32[]{:S(2)}, u32[]{:S(2)}) collective-permute-start(bf16[32,20,1024]{2,0,1:T(8,128)(2,1)} %collective-permute-done.3), channel_id=1, source_target_pairs={{0,1},{1,2},{2,3},{3,0},{4,5},{5,6},{6,7},{7,4},{8,9},{9,10},{10,1... | collective-permute-start | bytes 3932168 | tf_op jit(solution)/shard_map/ppermute | solution.py:86
  109.1 32.1 %collective-permute-start = (bf16[32,20,1024]{2,0,1:T(8,128)(2,1)}, bf16[32,20,1024]{2,0,1:T(8,128)(2,1)}, u32[]{:S(2)}, u32[]{:S(2)}) collective-permute-start(bf16[32,20,1024]{2,0,1:T(8,128)(2,1)} %copy.72), channel_id=1, source_target_pairs={{0,1},{1,2},{2,3},{3,0},{4,5},{5,6},{6,7},{7,4},{8,9},{9,10},{10,1... | collective-permute-start | bytes 3932168 | tf_op jit(solution)/shard_map/ppermute | solution.py:86
  111.2 58.1 %collective-permute-start.5 = (bf16[32,20,1024]{2,0,1:T(8,128)(2,1)}, bf16[32,20,1024]{2,0,1:T(8,128)(2,1)}, u32[]{:S(2)}, u32[]{:S(2)}) collective-permute-start(bf16[32,20,1024]{2,0,1:T(8,128)(2,1)} %collective-permute-done.4), channel_id=1, source_target_pairs={{0,1},{1,2},{2,3},{3,0},{4,5},{5,6},{6,7},{7,4},{8,9},{9,10},{10,1... | collective-permute-start | bytes 3932168 | tf_op jit(solution)/shard_map/ppermute | solution.py:86
  141.2 79.7 %collective-permute-start.1 = (bf16[32,20,1024]{2,0,1:T(8,128)(2,1)}, bf16[32,20,1024]{2,0,1:T(8,128)(2,1)}, u32[]{:S(2)}, u32[]{:S(2)}) collective-permute-start(bf16[32,20,1024]{2,0,1:T(8,128)(2,1)} %collective-permute-done), channel_id=1, source_target_pairs={{0,1},{1,2},{2,3},{3,0},{4,5},{5,6},{6,7},{7,4},{8,9},{9,10},{10,1... | collective-permute-start | bytes 3932168 | tf_op jit(solution)/shard_map/ppermute | solution.py:86
  220.9 156.5 %reduce-scatter.3.cloned.1.call-start = ((), (), s32[]{:S(2)}) async-start(), calls=%async_computation.6 | async-start | bytes 6553600 | tf_op jit(solution)/shard_map/reduce_scatter | solution.py:95
  220.9 52.9 %collective-permute-start.2 = (bf16[32,20,1024]{2,0,1:T(8,128)(2,1)}, bf16[32,20,1024]{2,0,1:T(8,128)(2,1)S(1)}, u32[]{:S(2)}, u32[]{:S(2)}) collective-permute-start(bf16[32,20,1024]{2,0,1:T(8,128)(2,1)} %collective-permute-done.1), channel_id=1, source_target_pairs={{0,1},{1,2},{2,3},{3,0},{4,5},{5,6},{6,7},{7,4},{8,9},{9,10},{10,1... | collective-permute-start | bytes 3932168 | tf_op jit(solution)/shard_map/ppermute | solution.py:86
  328.2 52.4 %all-to-all-start.3 = ((bf16[32,20,1024]{2,1,0:T(8,128)(2,1)}), bf16[32,20,1024]{2,1,0:T(8,128)(2,1)S(1)}, u32[]{:S(2)}, u32[]{:S(2)}) async-start(bf16[32,20,1024]{2,1,0:T(8,128)(2,1)} %convert_element_type.98), calls=%async_computation.5 | async-start | bytes 3145728 | tf_op jit(solution)/shard_map/all_to_all | solution.py:98
  380.6 87.8 %all-to-all-start.1 = ((bf16[32,20,1024]{2,1,0:T(8,128)(2,1)}), bf16[32,20,1024]{2,1,0:T(8,128)(2,1)S(1)}, u32[]{:S(2)}, u32[]{:S(2)}) async-start(bf16[32,20,1024]{2,1,0:T(8,128)(2,1)} %convert_element_type.90), calls=%async_computation.2 | async-start | bytes 3145728 | tf_op jit(solution)/shard_map/all_to_all | solution.py:98
Sparse Core Ops, SparseCore 0:
  221.0 75.8 reduce-scatter.4
  325.1 52.2 reduce-scatter.2
